TPU v7x, 512 devices: a whole 4x8x8 slice. The times are simulated.
512 devices in a mesh: owner: 64 (over y, x, core), rows: 8 (over z).
Axes of the slice: x: 4, y: 8, z: 8, core: 2. Of those that a mesh axis runs over, the one named last changes fastest.
Arguments:
- train_down: float32 [64, 1024, 2048], P('owner', None, 'rows'), may hold values from -0.1875 to 0.1875
- router_weight: float32 [2048, 64], P('rows', 'owner'), may hold values from -0.125 to 0.125
- router_gain: float32 [2048], P('rows'), may hold values from 0.25 to 1.75
Outputs:
- ready_down: bfloat16 [64, 2048, 1024], P('owner')
- serve_router: bfloat16 [2048, 64], replicated
All inputs are finite; a program needn't handle non-finite values.
Results may differ from a plain program's by a relative error of at most 0.001.
Values may be sent and summed in bfloat16 or wider, within the bound.
No kernel may reach another device: no remote copies, remote signals or barrier semaphores. Data moves between devices by JAX's collectives and lax.ppermute only.
A program may use at most 64 MiB of HBM per device.

v0:
```python
import jax
import jax.numpy as jnp
from jax import lax
from jax.sharding import PartitionSpec as P


def in_order(blocks, dim):
    blocks = jnp.moveaxis(blocks, 0, dim)
    dims = blocks.shape
    return blocks.reshape(*dims[:dim], dims[dim] * dims[dim + 1], *dims[dim + 2 :])


def from_everyone(array, axis):
    copies = jnp.broadcast_to(array, (lax.axis_size(axis), *array.shape))
    return lax.all_to_all(copies, axis, split_axis=0, concat_axis=0, tiled=True)


def gather_directly(array, axis, dim):
    return in_order(from_everyone(array, axis), dim)


def on_device(train_down, router_weight, router_gain):
    narrow_down = train_down.astype(jnp.bfloat16)
    ready_down = lax.all_gather(narrow_down, "rows", axis=2, tiled=True)
    ready_down = jnp.transpose(ready_down, (0, 2, 1))
    part_router = (router_weight * router_gain[:, None]).astype(jnp.bfloat16)
    row_router = lax.all_gather(part_router, "rows", axis=0, tiled=True)
    serve_router = gather_directly(row_router, "owner", 1)
    return (ready_down, serve_router)


def solution(mesh):
    in_specs = (P("owner", None, "rows"), P("rows", "owner"), P("rows"))
    out_specs = (P("owner", None, None), P())
    return jax.shard_map(
        on_device, mesh=mesh, in_specs=in_specs, out_specs=out_specs, check_vma=False
    )
```

profile of v0, /device:TPU:1, one launch (start us, length us, event | category | flops | bytes accessed | tf_op | source)
XLA Modules:
  0.0 85.6 jit_solution(9226915147789131716)
XLA Ops:
  7.2 0.0 all-gather.2.cloned.1.call-start
  7.2 2.2 %copy.7 = bf16[1,1024,256]{1,2,0:T(8,128)(2,1)} copy(f32[1,1024,256]{2,1,0:T(8,128)} %param.3) | data formatting | bytes 1572864 | tf_op args[0]
  9.4 0.0 all-gather.2.cloned.1.call-update
  9.5 0.7 multiply_convert_fusion
  10.2 19.4 %all_gather.9 = bf16[2048,1]{0,1:T(2,128)(2,1)S(1)} all-gather(bf16[256,1]{0,1:T(2,128)(2,1)S(1)} %multiply_convert_fusion), channel_id=1, replica_groups=mesh['owner'=64,'rows'=8] {'rows'}, dimensions={0}, use_global_device_ids=true | all-gather | bytes 4608 | tf_op jit(solution)/shard_map/all_gather | solution.py:27
  29.6 0.3 broadcast_bitcast_fusion
  29.9 0.5 broadcast.2
  30.4 2.2 %reduce.1 = bf16[64,2048]{1,0:T(8,128)(2,1)S(1)} reduce(bf16[64,1,2048]{2,1,0:T(2,128)(2,1)S(1)} %broadcast_bitcast_fusion, bf16[]{:T(256)} %broadcast.2), dimensions={1}, to_apply=%broadcast_bitcast_fusion.reduce_sub_computation | reduce | bytes 524290
  32.5 0.2 reshape.10
  32.7 27.4 %all_to_all.5 = bf16[64,2,1024]{2,1,0:T(2,128)(2,1)S(1)} all-to-all(bf16[64,2,1024]{2,1,0:T(2,128)(2,1)S(1)} %reshape.10), channel_id=1, replica_groups=mesh['owner'=64,'rows'=8] {'owner'}, dimensions={0} | all-to-all | bytes 524288 | tf_op jit(solution)/shard_map/all_to_all | solution.py:15
  60.2 0.2 reshape.11
  60.4 0.9 copy.10
  61.2 12.9 %all-gather.2.cloned.1.call-done = bf16[1,1024,2048]{1,2,0:T(8,128)(2,1)} async-done(((bf16[1,1024,256]{1,2,0:T(8,128)(2,1)}), bf16[1,1024,2048]{1,2,0:T(8,128)(2,1)}) %all-gather.2.cloned.1.call-update) | async-done | bytes 4194320 | tf_op jit(solution)/shard_map/all_gather | solution.py:24
  74.2 4.6 %copy.12 = bf16[1,2048,1024]{2,1,0:T(8,128)(2,1)} copy(bf16[1,2048,1024]{2,1,0:T(8,128)(2,1)} %bitcast.10) | data formatting | bytes 8388608
  (1 shorter events, 0.0 us)
Async XLA Ops:
  7.2 67.0 %all-gather.2.cloned.1.call-start = ((), (), s32[]{:S(2)}) async-start(), calls=%async_computation.1 | async-start | bytes 4718592 | tf_op jit(solution)/shard_map/all_gather | solution.py:24
Sparse Core Ops, SparseCore 0:
  10.6 63.4 all-gather.1
where the time goes:
time: 85.9 us; the launch traced here: 85.6 us
  blocking collectives  46.8 us (54%)
  between operations  14.1 us (16%)
  waiting for transfers between devices  12.9 us (15%)
  local copies, waits for them, and re-layouts  8.91 us (10%)
  other arithmetic  2.89 us (3%)
    all_to_all x1, blocking collectives, from_everyone(): return lax.all_to_all(copies, axis, split_axis=0, concat_axis=0, tiled=True)  27.4 us
    all_gather x1, blocking collectives, on_device(): row_router = lax.all_gather(part_router, 'rows', axis=0, tiled=True)  19.4 us
    all_gather x1, waiting for transfers between devices, on_device(): ready_down = lax.all_gather(narrow_down, 'rows', axis=2, tiled=True)  12.9 us
    unnamed x6, local copies, waits for them, and re-layouts  8.05 us
    unnamed x1, other arithmetic  2.15 us
  transfers between devices with their start and end apart: 1, of which 1 were waited for; matrix products, arithmetic and copies ran while one was open for 6% of the time, Pallas kernels for 0%

commit v1 on v0

--- a/solution.py
+++ b/solution.py
@@ -21,7 +21,9 @@
 
 def on_device(train_down, router_weight, router_gain):
     narrow_down = train_down.astype(jnp.bfloat16)
-    ready_down = lax.all_gather(narrow_down, "rows", axis=2, tiled=True)
+    ready_down = jnp.concatenate(
+        lax.all_to_all(jnp.stack([narrow_down] * lax.axis_size("rows")), "rows", 0, 0), axis=2
+    )
     ready_down = jnp.transpose(ready_down, (0, 2, 1))
     part_router = (router_weight * router_gain[:, None]).astype(jnp.bfloat16)
     row_router = lax.all_gather(part_router, "rows", axis=0, tiled=True)

time: 85.9 us -> 161 us (1.87)
  waiting for transfers between devices: 12.9 us -> 107 us
  blocking collectives: 46.8 us -> 19.4 us
  starting transfers between devices: 0.04 us -> 19.1 us
  between operations: 14.1 us -> 0.68 us
    all_to_all x0 -> x2, waiting for transfers between devices: none -> 107 us  [the longest x1 95.7 us: on_device(): lax.all_to_all(jnp.stack([narrow_down] * lax.axis_size('rows')), 'rows',...]
    all_to_all x1 -> x0, blocking collectives: 27.4 us -> none  [from_everyone(): return lax.all_to_all(copies, axis, split_axis=0, concat_axis=0, tiled=True)]
    all_to_all x0 -> x2, starting transfers between devices: none -> 19.1 us  [the longest x1 14.5 us: from_everyone(): return lax.all_to_all(copies, axis, split_axis=0, concat_axis=0, tiled=True)]
    all_gather x1 -> x0, waiting for transfers between devices: 12.9 us -> none  [on_device(): ready_down = lax.all_gather(narrow_down, 'rows', axis=2, tiled=True)]
    another operation x0 -> x1, local copies, waits for them, and re-layouts: none -> 2.55 us  [on_device(): jnp.stack([narrow_down] * lax.axis_size('rows'))]
    unnamed x6 -> x5, local copies, waits for them, and re-layouts: 8.05 us -> 6.55 us
  transfers between devices with their start and end apart: 1 -> 2, of which waited for: 1 -> 2; matrix products, arithmetic and copies ran while one was open for 6% -> 2% of each run, Pallas kernels for 0% -> 0%
where the time goes in v1:
time: 161 us
  waiting for transfers between devices  107 us (66%)
  blocking collectives  19.4 us (12%)
  starting transfers between devices  19.1 us (12%)
  local copies, waits for them, and re-layouts  10.2 us (6%)
  other arithmetic  4.17 us (3%)
    all_to_all x1, waiting for transfers between devices, on_device(): lax.all_to_all(jnp.stack([narrow_down] * lax.axis_size('rows')), 'rows',...  95.7 us
    all_gather x1, blocking collectives, on_device(): row_router = lax.all_gather(part_router, 'rows', axis=0, tiled=True)  19.4 us
    all_to_all x1, starting transfers between devices, from_everyone(): return lax.all_to_all(copies, axis, split_axis=0, concat_axis=0, tiled=True)  14.5 us
    all_to_all x1, waiting for transfers between devices, from_everyone(): return lax.all_to_all(copies, axis, split_axis=0, concat_axis=0, tiled=True)  11.6 us
    unnamed x5, local copies, waits for them, and re-layouts  6.55 us
    all_to_all x1, starting transfers between devices, on_device(): lax.all_to_all(jnp.stack([narrow_down] * lax.axis_size('rows')), 'rows',...  4.55 us
  transfers between devices with their start and end apart: 2, of which 2 were waited for; matrix products, arithmetic and copies ran while one was open for 2% of the time, Pallas kernels for 0%

profile of v1, /device:TPU:1, one launch (start us, length us, event | category | flops | bytes accessed | tf_op | source)
XLA Modules:
  0.0 160.8 jit_solution(14133238966752416072)
XLA Ops:
  0.6 0.7 multiply_convert_fusion
  1.3 19.4 %all_gather.5 = bf16[2048,1]{0,1:T(2,128)(2,1)S(1)} all-gather(bf16[256,1]{0,1:T(2,128)(2,1)S(1)} %multiply_convert_fusion), channel_id=1, replica_groups=mesh['owner'=64,'rows'=8] {'rows'}, dimensions={0}, use_global_device_ids=true | all-gather | bytes 4608 | tf_op jit(solution)/shard_map/all_gather | solution.py:29
  20.8 0.3 broadcast_bitcast_fusion
  21.0 0.5 broadcast.5
  21.6 2.2 %reduce.1 = bf16[64,2048]{1,0:T(8,128)(2,1)S(1)} reduce(bf16[64,1,2048]{2,1,0:T(2,128)(2,1)S(1)} %broadcast_bitcast_fusion, bf16[]{:T(256)} %broadcast.5), dimensions={1}, to_apply=%broadcast_bitcast_fusion.reduce_sub_computation | reduce | bytes 524290
  23.7 0.9 reshape.21
  24.6 14.5 %all-to-all-start.1 = ((bf16[64,2,1024]{2,1,0:T(2,128)(2,1)}), bf16[64,2,1024]{2,1,0:T(2,128)(2,1)S(1)}, u32[]{:S(2)}, u32[]{:S(2)}) async-start(bf16[64,2,1024]{2,1,0:T(2,128)(2,1)} %reshape.21), calls=%async_computation.1 | async-start | bytes 524288 | tf_op jit(solution)/shard_map/all_to_all | solution.py:15
  39.2 1.3 convert_bitcast_fusion
  40.4 0.2 copy.7
  40.6 11.6 %all-to-all-done.1 = bf16[64,2,1024]{2,1,0:T(2,128)(2,1)S(1)} async-done(((bf16[64,2,1024]{2,1,0:T(2,128)(2,1)}), bf16[64,2,1024]{2,1,0:T(2,128)(2,1)S(1)}, u32[]{:S(2)}, u32[]{:S(2)}) %all-to-all-start.1) | async-done | bytes 262176 | tf_op jit(solution)/shard_map/all_to_all | solution.py:15
  52.2 2.6 %stack.2 = bf16[8,1,1024,256]{2,3,1,0:T(8,128)(2,1)} broadcast(bf16[1024,256]{0,1:T(8,128)(2,1)S(1)} %copy.7), dimensions={2,3} | broadcast | bytes 4718592 | tf_op jit(solution)/shard_map/stack | solution.py:25
  54.8 4.5 %all-to-all-start = ((bf16[8,1,1024,256]{2,3,1,0:T(8,128)(2,1)}), bf16[8,1,1024,256]{2,3,1,0:T(8,128)(2,1)}, u32[]{:S(2)}, u32[]{:S(2)}) async-start(bf16[8,1,1024,256]{2,3,1,0:T(8,128)(2,1)} %stack.2), calls=%async_computation | async-start | bytes 8388608 | tf_op jit(solution)/shard_map/all_to_all | solution.py:25
  59.3 0.2 reshape.22
  59.6 0.9 copy.10
  60.4 95.7 %all-to-all-done = bf16[8,1,1024,256]{2,3,1,0:T(8,128)(2,1)} async-done(((bf16[8,1,1024,256]{2,3,1,0:T(8,128)(2,1)}), bf16[8,1,1024,256]{2,3,1,0:T(8,128)(2,1)}, u32[]{:S(2)}, u32[]{:S(2)}) %all-to-all-start) | async-done | bytes 4194336 | tf_op jit(solution)/shard_map/all_to_all | solution.py:25
  156.1 4.6 %copy.12 = bf16[1,2048,1024]{2,1,0:T(8,128)(2,1)} copy(bf16[1,2048,1024]{2,1,0:T(8,128)(2,1)} %bitcast.3) | data formatting | bytes 8388608
  (1 shorter events, 0.0 us)
Async XLA Ops:
  24.6 27.6 %all-to-all-start.1 = ((bf16[64,2,1024]{2,1,0:T(2,128)(2,1)}), bf16[64,2,1024]{2,1,0:T(2,128)(2,1)S(1)}, u32[]{:S(2)}, u32[]{:S(2)}) async-start(bf16[64,2,1024]{2,1,0:T(2,128)(2,1)} %reshape.21), calls=%async_computation.1 | async-start | bytes 524288 | tf_op jit(solution)/shard_map/all_to_all | solution.py:15
  54.8 101.4 %all-to-all-start = ((bf16[8,1,1024,256]{2,3,1,0:T(8,128)(2,1)}), bf16[8,1,1024,256]{2,3,1,0:T(8,128)(2,1)}, u32[]{:S(2)}, u32[]{:S(2)}) async-start(bf16[8,1,1024,256]{2,3,1,0:T(8,128)(2,1)} %stack.2), calls=%async_computation | async-start | bytes 8388608 | tf_op jit(solution)/shard_map/all_to_all | solution.py:25
